TPU v7x, 16 devices: a 4x2x1 block of a 4x4x8 slice. The times are simulated.
16 devices in a mesh: rep: 4 (over y, z, core), dp: 4 (over x).
Axes of the slice: x: 4, y: 2, z: 1, core: 2. Of those that a mesh axis runs over, the one named last changes fastest.
The devices are a block of a 4x4x8 slice.
Arguments:
- x: bfloat16 [16, 4096, 1024], P(('rep', 'dp')), parts along dimension 0
- dy: bfloat16 [16, 4096, 1024], P(('rep', 'dp')), parts along dimension 0
- w_gate: bfloat16 [2, 1024, 4096], P(None, 'dp')
- w_up: bfloat16 [2, 1024, 4096], P(None, 'dp')
- w_down: bfloat16 [2, 4096, 1024], P(None, 'dp')
- m_w_gate: float32 [2, 1024, 4096], P(None, 'dp')
- m_w_up: float32 [2, 1024, 4096], P(None, 'dp')
- m_w_down: float32 [2, 4096, 1024], P(None, 'dp')
- v_w_gate: float32 [2, 1024, 4096], P(None, 'dp')
- v_w_up: float32 [2, 1024, 4096], P(None, 'dp')
- v_w_down: float32 [2, 4096, 1024], P(None, 'dp')
Outputs:
- output 1: bfloat16 [8, 1024, 4096], P('rep', 'dp'), parts along dimension 0
- output 2: bfloat16 [8, 1024, 4096], P('rep', 'dp'), parts along dimension 0
- output 3: bfloat16 [8, 4096, 1024], P('rep', 'dp'), parts along dimension 0
- output 4: float32 [8, 1024, 4096], P('rep', 'dp'), parts along dimension 0
- output 5: float32 [8, 1024, 4096], P('rep', 'dp'), parts along dimension 0
- output 6: float32 [8, 4096, 1024], P('rep', 'dp'), parts along dimension 0
- output 7: float32 [8, 1024, 4096], P('rep', 'dp'), parts along dimension 0
- output 8: float32 [8, 1024, 4096], P('rep', 'dp'), parts along dimension 0
- output 9: float32 [8, 4096, 1024], P('rep', 'dp'), parts along dimension 0
There are 4 independent parts. A program takes and returns all parts, laid end to end along the dimension named above; an argument that names none is the same for every part.
All inputs are finite; a program needn't handle non-finite values.
Results may differ from a plain program's by a relative error of at most 0.0242.
Values are sent between devices in bfloat16 or wider.
A program may use at most 768 MiB of HBM per device.

v0:
```python
import jax
import jax.numpy as jnp
from jax import lax
from jax.sharding import PartitionSpec as P

NAMES = ("w_gate", "w_up", "w_down")


def matmul(a, w):
    return jnp.dot(a, w, preferred_element_type=jnp.float32).astype(jnp.bfloat16)


def normed(h):
    wide = h.astype(jnp.float32)
    scale = lax.rsqrt(jnp.mean(wide**2, -1, keepdims=True) + 1e-6)
    return (wide * scale).astype(jnp.bfloat16)


def layer(h, w):
    a = normed(h)
    gate = jnp.dot(a, w["w_gate"], preferred_element_type=jnp.float32)
    up = jnp.dot(a, w["w_up"], preferred_element_type=jnp.float32)
    return h + matmul((jax.nn.silu(gate) * up).astype(jnp.bfloat16), w["w_down"])


def adamw(w, m, v, g):
    m = 0.9 * m + 0.1 * g
    v = 0.95 * v + 0.05 * g * g
    step = m * lax.rsqrt(v + 1e-8) + 0.1 * w
    return (w - 0.02 * step).astype(jnp.bfloat16), m, v


def solution(mesh):
    def fetched(weights, number):
        return {name: lax.all_gather(w[number], "dp", axis=0, tiled=True) for name, w in zip(NAMES, weights, strict=True)}

    def step(x, dy, *arrays):
        weights, m, v = (arrays[i : i + 3] for i in (0, 3, 6))
        layers = weights[0].shape[0]
        h, kept = x[0], []
        for number in range(layers):
            kept.append(h)
            h = layer(h, fetched(weights, number))
        by_h, mine = dy[0], [None] * layers
        for number in reversed(range(layers)):
            _, back = jax.vjp(lambda w, h: layer(h, w), fetched(weights, number), kept[number])
            by_w, by_h = back(by_h)
            mine[number] = [lax.psum_scatter(by_w[name], "dp", scatter_dimension=0, tiled=True) for name in NAMES]
        gradients = [jnp.stack([mine[number][i] for number in range(layers)]).astype(jnp.float32) for i in range(3)]
        new = [adamw(w.astype(jnp.float32), m, v, g) for w, m, v, g in zip(weights, m, v, gradients, strict=True)]
        return tuple(one[which] for which in range(3) for one in new)

    states, cut = P(("rep", "dp"), None, None), P(None, "dp", None)
    return jax.shard_map(
        step,
        mesh=mesh,
        in_specs=(states, states) + (cut,) * 9,
        out_specs=(P("rep", "dp", None),) * 9,
        check_vma=False,
    )
```

profile of v0, /device:TPU:112, one launch (start us, length us, event | category | flops | bytes accessed | tf_op | source)
XLA Modules:
  0.0 1236.3 jit_solution(5384445598057429381)
XLA Ops:
  52.6 41.7 %all-gather.13.cloned.1.call-done = bf16[1,1024,4096]{2,1,0:T(8,128)(2,1)} async-done(((bf16[1,256,4096]{2,1,0:T(8,128)(2,1)}), bf16[1,1024,4096]{2,1,0:T(8,128)(2,1)}) %all-gather.13.cloned.1.call-update) | async-done | bytes 8388624 | tf_op jit(solution)/shard_map/all_gather | solution.py:35
  94.3 45.6 %fusion.54 = f32[4096,4096]{1,0:T(8,128)} fusion(bf16[1,1024,4096]{2,1,0:T(8,128)(2,1)} %all-gather.13.cloned.1.call-done, bf16[1,4096,1024]{1,2,0:T(8,128)(2,1)} %copy.20, f32[4096]{0:T(1024)S(1)} %add_rsqrt_fusion), kind=kOutput, calls=%fused_computation.83 | convolution fusion | flops 34372321280 | bytes 83902464 | tf_op jit(solution)/shard_map/dot_general | solution.py:21
  139.9 36.7 %all-gather.15.cloned.1.call-done = bf16[1,1024,4096]{2,1,0:T(8,128)(2,1)} async-done(((bf16[1,256,4096]{2,1,0:T(8,128)(2,1)}), bf16[1,1024,4096]{2,1,0:T(8,128)(2,1)}) %all-gather.15.cloned.1.call-update) | async-done | bytes 8388624 | tf_op jit(solution)/shard_map/all_gather | solution.py:35
  176.6 72.8 %multiply_convert_fusion.1 = (bf16[4096,4096]{1,0:T(8,128)(2,1)}, f32[4096,4096]{1,0:T(8,128)}) fusion(f32[4096,4096]{1,0:T(8,128)} %fusion.54, bf16[1,1024,4096]{2,1,0:T(8,128)(2,1)} %all-gather.15.cloned.1.call-done, bf16[1,4096,1024]{1,2,0:T(8,128)(2,1)} %copy.20, f32[4096]{0:T(1024)S(1)} %add_rsqrt_fusion), kind=kOutput, calls=%fused_computation.17 | convolution fusion | flops 34472984576 | bytes 184565760 | tf_op jit(solution)/shard_map/dot_general | solution.py:22
  258.9 43.0 %fusion.19 = (f32[4096]{0:T(1024)S(1)}, bf16[4096,1024]{0,1:T(8,128)(2,1)}) fusion(bf16[4096,4096]{1,0:T(8,128)(2,1)} %get-tuple-element.24, bf16[1,4096,1024]{2,1,0:T(8,128)(2,1)} %all-gather.17.cloned.1.call-done, bf16[1,4096,1024]{1,2,0:T(8,128)(2,1)} %copy.20), kind=kOutput, calls=%fused_computation.37 | convolution fusion | flops 34380705792 | bytes 58736640 | tf_op jit(solution)/shard_map/dot_general | solution.py:10
  302.6 38.5 %all-gather.23.cloned.1.call-done = bf16[1,1024,4096]{2,1,0:T(8,128)(2,1)} async-done(((bf16[1,256,4096]{2,1,0:T(8,128)(2,1)}), bf16[1,1024,4096]{2,1,0:T(8,128)(2,1)}) %all-gather.23.cloned.1.call-update) | async-done | bytes 8388624 | tf_op jit(solution)/shard_map/all_gather | solution.py:35
  341.1 46.0 %fusion.41 = f32[4096,4096]{1,0:T(8,128)} fusion(bf16[1,1024,4096]{2,1,0:T(8,128)(2,1)} %all-gather.23.cloned.1.call-done, bf16[4096,1024]{0,1:T(8,128)(2,1)} %get-tuple-element.27, f32[4096]{0:T(1024)S(1)} %fusion.76), kind=kOutput, calls=%fused_computation.70 | convolution fusion | flops 34372321280 | bytes 83902464 | tf_op jit(solution)/shard_map/jvp()/dot_general | solution.py:22
  387.1 36.1 %all-gather.21.cloned.1.call-done = bf16[1,4096,1024]{2,1,0:T(8,128)(2,1)} async-done(((bf16[1,1024,1024]{2,1,0:T(8,128)(2,1)}), bf16[1,4096,1024]{2,1,0:T(8,128)(2,1)}) %all-gather.21.cloned.1.call-update) | async-done | bytes 8388624 | tf_op jit(solution)/shard_map/all_gather | solution.py:35
  423.3 43.2 %convolution_convert_fusion.1 = bf16[4096,4096]{1,0:T(8,128)(2,1)} fusion(bf16[1,4096,1024]{2,1,0:T(8,128)(2,1)} %param.12, bf16[1,4096,1024]{2,1,0:T(8,128)(2,1)} %all-gather.21.cloned.1.call-done), kind=kOutput, calls=%fused_computation.25 | convolution fusion | flops 34376515584 | bytes 50331648 | tf_op jit(solution)/shard_map/transpose(jvp())/dot_general | solution.py:10
  466.5 38.9 %all-gather.19.cloned.1.call-done = bf16[1,1024,4096]{2,1,0:T(8,128)(2,1)} async-done(((bf16[1,256,4096]{2,1,0:T(8,128)(2,1)}), bf16[1,1024,4096]{2,1,0:T(8,128)(2,1)}) %all-gather.19.cloned.1.call-update) | async-done | bytes 8388624 | tf_op jit(solution)/shard_map/all_gather | solution.py:35
  505.4 84.0 %fusion.2 = (bf16[4096,4096]{1,0:T(8,128)(2,1)}, f32[4096,4096]{1,0:T(8,128)}) fusion(f32[4096,4096]{1,0:T(8,128)} %fusion.41, bf16[4096,4096]{1,0:T(8,128)(2,1)} %convolution_convert_fusion.1, bf16[1,1024,4096]{2,1,0:T(8,128)(2,1)} %all-gather.19.cloned.1.call-done, bf16[4096,1024]{0,1:T(8,128)(2,1)} %get-tuple-element.27, f32[4096]{0:T(1024)S(1)} %fusion.76), kind=kOutput, calls=%fused_computation.8 | convolution fusion | flops 34573647872 | bytes 218120192 | tf_op jit(solution)/shard_map/jvp()/dot_general | solution.py:21
  589.4 42.9 %fusion.45 = bf16[4096,1024]{0,1:T(8,128)(2,1)} fusion(bf16[4096,4096]{1,0:T(8,128)(2,1)} %get-tuple-element.28, bf16[1,1024,4096]{2,1,0:T(8,128)(2,1)} %all-gather.19.cloned.1.call-done), kind=kOutput, calls=%fused_computation.74 | convolution fusion | flops 34359738368 | bytes 50331648 | tf_op jit(solution)/shard_map/transpose(jvp())/dot_general | solution.py:21
  632.3 52.7 %fusion.21 = (f32[4096]{0:T(1024)S(1)}, bf16[4096,1024]{0,1:T(8,128)(2,1)}) fusion(bf16[4096,1024]{0,1:T(8,128)(2,1)} %get-tuple-element.27, bf16[4096,1024]{0,1:T(8,128)(2,1)} %fusion.45, bf16[1,1024,4096]{2,1,0:T(8,128)(2,1)} %all-gather.23.cloned.1.call-done, bf16[4096,4096]{1,0:T(8,128)(2,1)} %convolution_convert_fusion.1, ...), kind=kOutput, calls=%fused_computation.39 | convolution fusion | flops 34485563392 | bytes 134234112 | tf_op jit(solution)/shard_map/transpose(jvp())/dot_general | solution.py:22
  698.9 42.6 %convolution_convert_fusion.3 = bf16[4096,1024]{1,0:T(8,128)(2,1)} fusion(bf16[4096,4096]{1,0:T(8,128)(2,1)} %get-tuple-element.24, bf16[4096,1024]{0,1:T(8,128)(2,1)} %fusion.38), kind=kOutput, calls=%fused_computation.92 | convolution fusion | flops 34363932672 | bytes 50331648 | tf_op jit(solution)/shard_map/transpose(jvp())/dot_general | solution.py:10
  741.6 53.1 %fusion.58 = bf16[4096,1024]{1,0:T(8,128)(2,1)} fusion(bf16[1,4096,1024]{2,1,0:T(8,128)(2,1)} %param.12, f32[4096,4096]{1,0:T(8,128)} %fusion.41, f32[4096,4096]{1,0:T(8,128)} %get-tuple-element.29), kind=kOutput, calls=%fused_computation.87 | convolution fusion | flops 34464595968 | bytes 150994944 | tf_op jit(solution)/shard_map/transpose(jvp())/dot_general | solution.py:10
  794.9 43.2 %convolution_convert_fusion = bf16[4096,4096]{1,0:T(8,128)(2,1)} fusion(bf16[4096,1024]{0,1:T(8,128)(2,1)} %fusion.38, bf16[1,4096,1024]{2,1,0:T(8,128)(2,1)} %all-gather.17.cloned.1.call-done), kind=kOutput, calls=%fused_computation.24 | convolution fusion | flops 34376515584 | bytes 50331648 | tf_op jit(solution)/shard_map/transpose(jvp())/dot_general | solution.py:10
  838.1 46.5 %fusion.67 = bf16[1024,4096]{1,0:T(8,128)(2,1)} fusion(bf16[4096,4096]{1,0:T(8,128)(2,1)} %convolution_convert_fusion, f32[4096,4096]{1,0:T(8,128)} %fusion.54, bf16[1,4096,1024]{1,2,0:T(8,128)(2,1)} %copy.20, f32[4096]{0:T(1024)S(1)} %copy-done.7), kind=kOutput, calls=%fused_computation.91 | convolution fusion | flops 34477178880 | bytes 117456896 | tf_op jit(solution)/shard_map/transpose(jvp())/dot_general | solution.py:22
  885.3 46.3 %fusion.66 = bf16[1024,4096]{1,0:T(8,128)(2,1)} fusion(bf16[4096,4096]{1,0:T(8,128)(2,1)} %convolution_convert_fusion.1, bf16[4096,1024]{0,1:T(8,128)(2,1)} %get-tuple-element.27, f32[4096]{0:T(1024)S(1)} %copy-done.2, f32[4096,4096]{1,0:T(8,128)} %get-tuple-element.29), kind=kOutput, calls=%fused_computation.90 | convolution fusion | flops 34477178880 | bytes 117456896 | tf_op jit(solution)/shard_map/transpose(jvp())/dot_general | solution.py:22
  931.7 65.7 %fusion.63 = bf16[1024,4096]{1,0:T(8,128)(2,1)} fusion(f32[4096,4096]{1,0:T(8,128)} %fusion.54, f32[4096,4096]{1,0:T(8,128)} %get-tuple-element.25, bf16[4096,4096]{1,0:T(8,128)(2,1)} %convolution_convert_fusion, bf16[1,4096,1024]{1,2,0:T(8,128)(2,1)} %copy.20, f32[4096]{0:T(1024)S(1)} %copy-done.7), kind=kOutput, calls=%fused_computation.88 | convolution fusion | flops 34561064960 | bytes 184565760 | tf_op jit(solution)/shard_map/transpose(jvp())/dot_general | solution.py:21
  998.1 42.6 %convolution_convert_fusion.2 = bf16[1024,4096]{1,0:T(8,128)(2,1)} fusion(bf16[4096,4096]{1,0:T(8,128)(2,1)} %get-tuple-element.28, bf16[4096,1024]{0,1:T(8,128)(2,1)} %get-tuple-element.27, f32[4096]{0:T(1024)S(1)} %copy-done.3), kind=kOutput, calls=%fused_computation.89 | convolution fusion | flops 34372321280 | bytes 50348032 | tf_op jit(solution)/shard_map/transpose(jvp())/dot_general | solution.py:21
  1055.7 15.0 %fusion.29 = (bf16[2,256,4096]{2,1,0:T(8,128)(2,1)}, f32[2,256,4096]{2,1,0:T(8,128)}, f32[2,256,4096]{2,1,0:T(8,128)}) fusion(bf16[2,256,4096]{2,1,0:T(8,128)(2,1)} %param.14, bf16[1,256,4096]{2,1,0:T(8,128)(2,1)} %bitcast.83, bf16[1,256,4096]{2,1,0:T(8,128)(2,1)} %bitcast.82, f32[2,256,4096]{2,1,0:T(8,128)} %param.20, f32[2,256,4096]{2,1,0:T(8,128)} %param.17), kind=kLoop, calls=%fused_computation.58 | loop fusion | flops 39845888 | bytes 46137344 | tf_op jit(solution)/shard_map/convert_element_type | solution.py:30
  1070.7 64.1 %reduce-scatter.7.cloned.1.call-done = bf16[256,4096]{1,0:T(8,128)(2,1)} async-done(((bf16[1024,4096]{1,0:T(8,128)(2,1)}), bf16[256,4096]{1,0:T(8,128)(2,1)}) %reduce-scatter.7.cloned.1.call-update) | async-done | bytes 2097168 | tf_op jit(solution)/shard_map/reduce_scatter | solution.py:48
  1134.8 78.9 %reduce-scatter.9.cloned.1.call-done = bf16[256,4096]{1,0:T(8,128)(2,1)} async-done(((bf16[1024,4096]{1,0:T(8,128)(2,1)}), bf16[256,4096]{1,0:T(8,128)(2,1)}) %reduce-scatter.9.cloned.1.call-update) | async-done | bytes 2097168 | tf_op jit(solution)/shard_map/reduce_scatter | solution.py:48
  1213.7 15.3 %fusion.25 = (bf16[2,256,4096]{2,1,0:T(8,128)(2,1)}, f32[2,256,4096]{2,1,0:T(8,128)}, f32[2,256,4096]{2,1,0:T(8,128)}) fusion(bf16[2,256,4096]{2,1,0:T(8,128)(2,1)} %param.13, bf16[1,256,4096]{2,1,0:T(8,128)(2,1)} %bitcast.85, bf16[1,256,4096]{2,1,0:T(8,128)(2,1)} %bitcast.84, f32[2,256,4096]{2,1,0:T(8,128)} %param.19, f32[2,256,4096]{2,1,0:T(8,128)} %param.16), kind=kLoop, calls=%fused_computation.54 | loop fusion | flops 39845888 | bytes 46137344 | tf_op jit(solution)/shard_map/convert_element_type | solution.py:30
  (56 shorter events, 86.1 us)
Async XLA Ops:
  7.2 87.1 %all-gather.13.cloned.1.call-start = ((), (), s32[]{:S(2)}) async-start(), calls=%async_computation.12 | async-start | bytes 10485760 | tf_op jit(solution)/shard_map/all_gather | solution.py:35
  12.0 164.6 %all-gather.15.cloned.1.call-start = ((), (), s32[]{:S(2)}) async-start(), calls=%async_computation.13 | async-start | bytes 10485760 | tf_op jit(solution)/shard_map/all_gather | solution.py:35
  16.9 242.0 %all-gather.17.cloned.1.call-start = ((), (), s32[]{:S(2)}) async-start(), calls=%async_computation.14 | async-start | bytes 10485760 | tf_op jit(solution)/shard_map/all_gather | solution.py:35
  21.7 319.4 %all-gather.23.cloned.1.call-start = ((), (), s32[]{:S(2)}) async-start(), calls=%async_computation.17 | async-start | bytes 10485760 | tf_op jit(solution)/shard_map/all_gather | solution.py:35
  22.4 400.9 %all-gather.21.cloned.1.call-start = ((), (), s32[]{:S(2)}) async-start(), calls=%async_computation.16 | async-start | bytes 10485760 | tf_op jit(solution)/shard_map/all_gather | solution.py:35
  23.0 482.4 %all-gather.19.cloned.1.call-start = ((), (), s32[]{:S(2)}) async-start(), calls=%async_computation.15 | async-start | bytes 10485760 | tf_op jit(solution)/shard_map/all_gather | solution.py:35
  23.6 1017.1 %reduce-scatter.15.cloned.1.call-start = ((), (), s32[]{:S(2)}) async-start(), calls=%async_computation.10 | async-start | bytes 10485760 | tf_op jit(solution)/shard_map/reduce_scatter | solution.py:48
  40.7 135.9 %copy-start.6 = (f32[4096]{0:T(1024)}, f32[4096]{0:T(1024)S(1)}, u32[]{:S(2)}) copy-start(f32[4096]{0:T(1024)S(1)} %add_rsqrt_fusion) | copy-start | bytes 49156
  302.0 0.6 copy-start.4
  302.6 202.8 %copy-start = (f32[4096]{0:T(1024)}, f32[4096]{0:T(1024)S(1)}, u32[]{:S(2)}) copy-start(f32[4096]{0:T(1024)S(1)} %fusion.76) | copy-start | bytes 49156
  632.3 52.8 %copy-start.5 = (f32[4096]{0:T(1024)S(1)}, f32[4096]{0:T(1024)}, u32[]{:S(2)}) copy-start(f32[4096]{0:T(1024)} %copy-done.4) | copy-start | bytes 49156
  632.3 52.8 %copy-start.1 = (f32[4096]{0:T(1024)S(1)}, f32[4096]{0:T(1024)}, u32[]{:S(2)}) copy-start(f32[4096]{0:T(1024)} %copy-done) | copy-start | bytes 49156
  741.6 299.2 %reduce-scatter.17.cloned.1.call-start = ((), (), s32[]{:S(2)}) async-start(), calls=%async_computation.11 | async-start | bytes 10485760 | tf_op jit(solution)/shard_map/reduce_scatter | solution.py:48
  794.8 43.3 %copy-start.7 = (f32[4096]{0:T(1024)S(1)}, f32[4096]{0:T(1024)}, u32[]{:S(2)}) copy-start(f32[4096]{0:T(1024)} %copy-done.6) | copy-start | bytes 49156
  794.8 260.8 %reduce-scatter.11.cloned.1.call-start = ((), (), s32[]{:S(2)}) async-start(), calls=%async_computation.8 | async-start | bytes 10485760 | tf_op jit(solution)/shard_map/reduce_scatter | solution.py:48
  884.6 0.7 copy-start.2
  884.6 171.0 %reduce-scatter.13.cloned.1.call-start = ((), (), s32[]{:S(2)}) async-start(), calls=%async_computation.9 | async-start | bytes 10485760 | tf_op jit(solution)/shard_map/reduce_scatter | solution.py:48
  931.6 203.2 %reduce-scatter.7.cloned.1.call-start = ((), (), s32[]{:S(2)}) async-start(), calls=%async_computation.6 | async-start | bytes 10485760 | tf_op jit(solution)/shard_map/reduce_scatter | solution.py:48
  997.4 0.7 copy-start.3
  997.5 216.3 %reduce-scatter.9.cloned.1.call-start = ((), (), s32[]{:S(2)}) async-start(), calls=%async_computation.7 | async-start | bytes 10485760 | tf_op jit(solution)/shard_map/reduce_scatter | solution.py:48
Sparse Core Ops, SparseCore 0:
  12.2 82.1 all-gather.12
  96.4 80.1 all-gather.14
  178.8 80.1 all-gather.16
  260.9 80.1 all-gather.22
  343.1 80.1 all-gather.20
  425.2 80.1 all-gather.18
  741.7 77.2 reduce-scatter.14
  821.4 76.1 reduce-scatter.16
  900.5 76.1 reduce-scatter.10
  979.5 76.1 reduce-scatter.12
  1058.6 76.1 reduce-scatter.6
  1137.6 76.1 reduce-scatter.8
where the time goes:
time: 1250 us; the launch traced here: 1240 us
  matrix products  770 us (62%)
  waiting for transfers between devices  347 us (28%)
  other arithmetic  64.1 us (5%)
  local copies, waits for them, and re-layouts  39.8 us (3%)
  between operations  14.8 us (1%)
    dot_general x5, matrix products, layer(): gate = jnp.dot(a, w['w_gate'], preferred_element_type=jnp.float32)  281 us
    dot_general x5, matrix products, layer(): up = jnp.dot(a, w['w_up'], preferred_element_type=jnp.float32)  264 us
    dot_general x5, matrix products, matmul(): jnp.dot(a, w, preferred_element_type=jnp.float32).astype(jnp.bfloat16)  225 us
    all_gather x6, waiting for transfers between devices, fetched(): lax.all_gather(w[number], 'dp', axis=0, tiled=True)  201 us
    reduce_scatter x6, waiting for transfers between devices, step(): lax.psum_scatter(by_w[name], 'dp', scatter_dimension=0, tiled=True)  143 us
    convert_element_type x3, other arithmetic, adamw(): return ((w - 0.02 * step).astype(jnp.bfloat16), m, v)  45.1 us
    unnamed x18, local copies, waits for them, and re-layouts  25.6 us
  transfers between devices with their start and end apart: 12, of which 8 were waited for; matrix products, arithmetic and copies ran while one was open for 50% of the time, Pallas kernels for 0%

commit v1 on v0

v1 whole, which is shorter than its diff:
```python
import functools

import jax
import jax.numpy as jnp
from jax import lax
from jax.experimental import pallas as pl
from jax.experimental.pallas import tpu as pltpu
from jax.sharding import PartitionSpec as P

F32, BF16 = jnp.float32, jnp.bfloat16
VMEM_LIMIT = 61 * 2**20
CHUNKS = 4
LAST_RANGES = ((0, 1), (1, 2), (2, 3), (3, 4))


def dot(a, b, over_a, over_b):
    return lax.dot_general(a, b, (((over_a,), (over_b,)), ((), ())), preferred_element_type=F32)


def rounded(a):
    return a.astype(BF16).astype(F32)


def norm_scale(wide):
    return lax.rsqrt(jnp.mean(wide * wide, -1, keepdims=True) + 1e-6)


def riding(kernel, ins, outs, gather, steps, when):
    def whole(*refs):
        refs = list(refs)
        take = lambda n: [refs.pop(0) for _ in range(n)]
        mine, sources, results, gathered = take(ins), take(3), take(outs), take(gather.count)
        sems = [refs.pop(), refs.pop()]
        gather.bind(sources, gathered, sems[::-1])
        index = 0
        for axis in range(len(steps)):
            index = index * steps[axis] + pl.program_id(axis)
        total = 1
        for n in steps:
            total *= n
        pl.when(index == 0)(gather.begin)
        if when[0] < total:
            pl.when(index == when[0])(gather.pass_on)
        if when[1] < total:
            pl.when(index == when[1])(gather.pass_far)
        kernel(*mine, *results, *refs)

        @pl.when(index == total - 1)
        def _():
            if when[0] >= total:
                gather.pass_on()
            if when[1] >= total:
                gather.pass_far()
            gather.end()

    return whole


def call(kernel, grid, in_specs, out_specs, out_shape, flops, moved, scratch=(), aliases=None, name=None, gather=None, when=None, ident=None, sources=None):
    params = dict(vmem_limit_bytes=VMEM_LIMIT)
    in_specs, out_specs, out_shape, scratch = list(in_specs), out_specs, out_shape, list(scratch)
    if gather is not None:
        kernel = riding(kernel, len(in_specs), len(out_specs), gather, grid, when)
        in_specs = in_specs + [ANY] * 3
        out_specs = list(out_specs) + [ANY] * gather.count
        out_shape = list(out_shape) + gather.out_shape(sources[0].shape[1], sources[2].shape[2])
        scratch = scratch + gather.scratch()
        params.update(collective_id=ident, has_side_effects=True)
    run = pl.pallas_call(
        kernel,
        grid=grid,
        in_specs=in_specs,
        out_specs=out_specs,
        out_shape=out_shape,
        scratch_shapes=scratch,
        input_output_aliases=aliases or {},
        name=name,
        cost_estimate=pl.CostEstimate(flops=int(flops), bytes_accessed=int(moved), transcendentals=0),
        compiler_params=pltpu.CompilerParams(**params),
    )
    return run if gather is None else lambda *operands: run(*operands, *sources)


MESH = pl.DeviceIdType.MESH
ANY = pl.BlockSpec(memory_space=pl.ANY)
UNITS = 4


class Gather:
    def __init__(self, pieces, group):
        self.pieces, self.group = pieces, group
        self.count = len(pieces)

    def out_shape(self, rows, width):
        return [jax.ShapeDtypeStruct((self.group * rows, width), BF16)] * self.count

    def scratch(self):
        return [pltpu.SemaphoreType.DMA((self.count, 16)), pltpu.SemaphoreType.DMA((self.count, 16))] if self.count else []

    def bind(self, sources, outs, sems):
        self.sources, self.outs = sources, outs
        self.send, self.recv = sems
        me, n = lax.axis_index("dp"), self.group
        rep = lax.axis_index("rep")
        self.core = lax.rem(rep, 2)
        self.me, self.right, self.left = me, lax.rem(me + 1, n), lax.rem(me + n - 1, n)
        self.to_right, self.to_left = {"dp": self.right}, {"dp": self.left}
        self.to_other = {"rep": rep + 1 - 2 * self.core}

    def source(self, k, unit):
        which, layer, chunk, tall = self.pieces[k]
        ref, out = self.sources[which], self.outs[k]
        rows, width = out.shape[0] // self.group, out.shape[1] // UNITS
        if tall:
            return ref.at[layer, pl.ds(chunk * rows, rows), pl.ds(pl.multiple_of(unit * width, width), width)]
        return ref.at[layer, :, pl.ds(pl.multiple_of((unit * CHUNKS + chunk) * width, width), width)]

    def place(self, k, owner, unit):
        out = self.outs[k]
        rows, width = out.shape[0] // self.group, out.shape[1] // UNITS
        return out.at[pl.ds(pl.multiple_of(owner * rows, rows), rows), pl.ds(pl.multiple_of(unit * width, width), width)]

    def copy(self, k, slot, source, target, device):
        return pltpu.make_async_remote_copy(
            src_ref=source, dst_ref=target, send_sem=self.send.at[k, slot], recv_sem=self.recv.at[k, slot], device_id=device, device_id_type=MESH
        )

    def own(self, k):
        return [self.copy(k, u, self.source(k, u), self.place(k, self.me, u), self.to_other) for u in range(UNITS)]

    def near(self, k):
        sends = []
        for u in range(2):
            unit = 2 * self.core + u
            sends.append(self.copy(k, 4 + u, self.source(k, unit), self.place(k, self.me, unit), self.to_right))
            sends.append(self.copy(k, 6 + u, self.source(k, unit), self.place(k, self.me, unit), self.to_left))
        return sends

    def on(self, k):
        first, second = 2 * self.core, 2 * self.core + 1
        from_left, from_right = self.place(k, self.left, first), self.place(k, self.right, second)
        return [self.copy(k, 12, from_left, from_left, self.to_right), self.copy(k, 13, from_right, from_right, self.to_left)]

    def across(self, k):
        sends = []
        for u in range(2):
            for slot, owner in ((8, self.left), (10, self.right)):
                block = self.place(k, owner, 2 * self.core + u)
                sends.append(self.copy(k, slot + u, block, block, self.to_other))
        return sends

    def across_far(self, k):
        far = lax.rem(self.me + 2, self.group)
        return [self.copy(k, 14 + u, b, b, self.to_other) for u in range(2) for b in [self.place(k, far, 2 * self.core + u)]]

    def begin(self):
        barrier = pltpu.get_barrier_semaphore()
        for device in (self.to_right, self.to_left, self.to_other):
            pl.semaphore_signal(barrier, inc=1, device_id=device, device_id_type=MESH)
        pl.semaphore_wait(barrier, 3)
        for k in range(self.count):
            for copy in self.near(k):
                copy.start()
        for k in range(self.count):
            for copy in self.own(k):
                copy.start()

    def pass_on(self):
        for k in range(self.count):
            for copy in self.near(k):
                copy.wait_recv()
            for copy in self.on(k):
                copy.start()
            for copy in self.across(k):
                copy.start()

    def pass_far(self):
        for k in range(self.count):
            for copy in self.on(k):
                copy.wait_recv()
            for copy in self.across_far(k):
                copy.start()

    def end(self):
        for k in range(self.count):
            for copies in (self.own(k), self.across(k), self.across_far(k)):
                for copy in copies:
                    copy.wait_recv()
            for copies in (self.own(k), self.near(k), self.on(k), self.across(k), self.across_far(k)):
                for copy in copies:
                    copy.wait_send()


def once(shape, index):
    return pl.BlockSpec(shape, index, pipeline_mode=pl.Buffered(1))


def nothing_kernel():
    pass


def fetch(gather, ident, sources):
    return call(nothing_kernel, (1,), [], [], [], 10**9, 10**7, name="fetch", gather=gather, when=(1, 1), ident=ident, sources=sources)()


def gate_up_kernel(first, h, wg, wu, *refs):
    if first:
        a_out, p, gate, up, a = refs
        wide = h[...].astype(F32)
        a[...] = (wide * norm_scale(wide)).astype(BF16)
        a_out[...] = a[...]
    else:
        p, gate, up = refs
        a = h
    half = wg.shape[1] // 2
    for part in range(2):
        cols = pl.ds(part * half, half)
        g = dot(a[...], wg[:, cols], 1, 0)
        u = dot(a[...], wu[:, cols], 1, 0)
        gate[:, cols] = g
        up[:, cols] = u
        p[:, cols] = (g * jax.nn.sigmoid(g) * u).astype(BF16)


def gate_up(first, h, wg, wu, **extra):
    t, d = h.shape
    f = wg.shape[1]
    tm = min(t, 512)
    token = pl.BlockSpec((tm, d), lambda i: (i, 0))
    tile = pl.BlockSpec((tm, f), lambda i: (i, 0))
    whole = once((d, f), lambda i: (0, 0))
    return call(
        functools.partial(gate_up_kernel, first),
        (t // tm,),
        [token, whole, whole],
        [token] * first + [tile, tile, tile],
        [jax.ShapeDtypeStruct((t, d), BF16)] * first + [jax.ShapeDtypeStruct((t, f), BF16)] + [jax.ShapeDtypeStruct((t, f), F32)] * 2,
        4 * t * d * f,
        10 * t * f,
        [pltpu.VMEM((tm, d), BF16)] * first,
        name="gate_up",
        **extra,
    )(h, wg, wu)


def down_kernel(pieces, h, *refs):
    ps, ws, (h_out, a_out) = refs[:pieces], refs[pieces : 2 * pieces], refs[2 * pieces :]
    total = dot(ps[0][...], ws[0][...], 1, 0)
    for p, w in zip(ps[1:], ws[1:]):
        total = total + dot(p[...], w[...], 1, 0)
    new = (h[...].astype(F32) + rounded(total)).astype(BF16)
    h_out[...] = new
    wide = new.astype(F32)
    a_out[...] = (wide * norm_scale(wide)).astype(BF16)


def down(ps, ws, h, **extra):
    t, d = h.shape
    n, f = len(ps), ps[0].shape[1]
    tm = min(t, 512)
    token = pl.BlockSpec((tm, d), lambda i: (i, 0))
    return call(
        functools.partial(down_kernel, n),
        (t // tm,),
        [token] + [pl.BlockSpec((tm, f), lambda i: (i, 0))] * n + [once((f, d), lambda i: (0, 0))] * n,
        [token, token],
        [jax.ShapeDtypeStruct((t, d), BF16)] * 2,
        2 * t * d * f * n,
        2 * t * f * n,
        name="down",
        **extra,
    )(h, *ps, *ws)


def hidden_gradients(g, u, dp):
    s = jax.nn.sigmoid(g)
    silu = g * s
    return silu, dp * u * (s * (1 + g * (1 - s))), dp * silu


def hidden_kernel(a, dy, wg, wu, wd, p, dg, du):
    half = wg.shape[1] // 2
    for part in range(2):
        cols = pl.ds(part * half, half)
        g = dot(a[...], wg[:, cols], 1, 0)
        u = dot(a[...], wu[:, cols], 1, 0)
        dp = rounded(dot(dy[...], wd[cols, :], 1, 1))
        silu, by_g, by_u = hidden_gradients(g, u, dp)
        p[:, cols] = (silu * u).astype(BF16)
        dg[:, cols] = by_g.astype(BF16)
        du[:, cols] = by_u.astype(BF16)


def hidden(a, dy, wg, wu, wd, **extra):
    t, d = a.shape
    f = wg.shape[1]
    tm = min(t, 1024 if extra.get("gather") is None else 512)
    token = pl.BlockSpec((tm, d), lambda i: (i, 0))
    tile = pl.BlockSpec((tm, f), lambda i: (i, 0))
    whole = lambda shape: once(shape, lambda i: (0, 0))
    return call(
        hidden_kernel,
        (t // tm,),
        [token, token, whole((d, f)), whole((d, f)), whole((f, d))],
        [tile] * 3,
        [jax.ShapeDtypeStruct((t, f), BF16)] * 3,
        6 * t * d * f,
        6 * t * f,
        name="hidden",
        **extra,
    )(a, dy, wg, wu, wd)


def hidden_back_kernel(dh, wd, gate, up, dg, du):
    half = wd.shape[0] // 2
    for part in range(2):
        cols = pl.ds(part * half, half)
        dp = rounded(dot(dh[...], wd[cols, :], 1, 1))
        _, by_g, by_u = hidden_gradients(gate[:, cols], up[:, cols], dp)
        dg[:, cols] = by_g.astype(BF16)
        du[:, cols] = by_u.astype(BF16)


def hidden_back(dh, wd, gate, up):
    t, d = dh.shape
    f = wd.shape[0]
    tm = min(t, 512)
    token = pl.BlockSpec((tm, d), lambda i: (i, 0))
    tile = pl.BlockSpec((tm, f), lambda i: (i, 0))
    return call(
        hidden_back_kernel,
        (t // tm,),
        [token, once((f, d), lambda i: (0, 0)), tile, tile],
        [tile] * 2,
        [jax.ShapeDtypeStruct((t, f), BF16)] * 2,
        2 * t * d * f,
        12 * t * f,
        name="hidden_back",
    )(dh, wd, gate, up)


def by_weights_kernel(n, halves, dy, a, *refs):
    ps, dgs, dus = (refs[k * n : k * n + n] for k in range(3))
    out, acc_d, acc_g, acc_u = refs[3 * n :]
    chunk, i = pl.program_id(0) // halves, pl.program_id(1)
    half = lax.rem(pl.program_id(0), halves)
    group, rows = out.shape[0], out.shape[3]
    for c in range(n):

        @pl.when(chunk == c)
        def _():
            terms = dot(ps[c][...], dy[...], 0, 0), dot(a[...], dgs[c][...], 0, 0), dot(a[...], dus[c][...], 0, 0)

            @pl.when(i == 0)
            def _():
                for acc, term in zip((acc_d, acc_g, acc_u), terms):
                    acc[...] = term

            @pl.when(i > 0)
            def _():
                by_d, by_g, by_u = ((acc[...] + term).astype(BF16) for acc, term in zip((acc_d, acc_g, acc_u), terms))
                part = group // halves
                out[pl.ds(half * part, part), 0, 0] = by_d.reshape(part, rows, by_d.shape[1])
                width = by_g.shape[1]
                for h in range(halves):

                    @pl.when(half == h)
                    def _():
                        out[:, 0, 1, :, pl.ds(h * width, width)] = by_g.reshape(group, rows, width)
                        out[:, 0, 2, :, pl.ds(h * width, width)] = by_u.reshape(group, rows, width)


def by_weights(ps, dgs, dus, dy, a, group):
    t, d = a.shape
    n, f = len(ps), ps[0].shape[1]
    halves, steps = 2, 2
    tm, width = t // steps, f // halves
    token = pl.BlockSpec((tm, d), lambda j, i: (i, 0))

    def tile(c):
        def index(j, i):
            before, after = j < c * halves, j >= (c + 1) * halves
            row = jnp.where(before, 0, jnp.where(after, steps - 1, i))
            return row, jnp.where(before, 0, jnp.where(after, halves - 1, j - c * halves))

        return pl.BlockSpec((tm, width), index if n > 1 else lambda j, i: (i, j))

    return call(
        functools.partial(by_weights_kernel, n, halves),
        (n * halves, steps),
        [token, token] + [tile(c) for c in range(n)] * 3,
        pl.BlockSpec((group, 1, 3, d // group, f), lambda j, i: (0, j // halves, 0, 0, 0)),
        jax.ShapeDtypeStruct((group, n, 3, d // group, f), BF16),
        6 * t * d * f * n,
        10 * t * f * n,
        [pltpu.VMEM((width, d), F32)] + [pltpu.VMEM((d, width), F32)] * 2,
        name="by_weights",
    )(dy, a, *ps, *dgs, *dus)


def by_input_kernel(n, h, dy, *refs):
    dgs, dus, wgs, wus = (refs[k * n : k * n + n] for k in range(4))
    out = refs[4 * n]

    def back(parts, ws):
        total = dot(parts[0][...], ws[0][...], 1, 1)
        for part, w in zip(parts[1:], ws[1:]):
            total = total + dot(part[...], w[...], 1, 1)
        return rounded(total)

    da = rounded(back(dgs, wgs) + back(dus, wus))
    wide = h[...].astype(F32)
    scale = norm_scale(wide)
    by_scale = jnp.sum(da * wide, -1, keepdims=True)
    by_wide = da * scale - (by_scale * scale * scale * scale / wide.shape[-1]) * wide
    out[...] = (dy[...].astype(F32) + rounded(by_wide)).astype(BF16)


def by_input(h, dy, dgs, dus, wgs, wus):
    t, d = h.shape
    n, f = len(dgs), dgs[0].shape[1]
    tm = min(t, 512)
    token = pl.BlockSpec((tm, d), lambda i: (i, 0))
    return call(
        functools.partial(by_input_kernel, n),
        (t // tm,),
        [token, token] + [pl.BlockSpec((tm, f), lambda i: (i, 0))] * (2 * n) + [once((d, f), lambda i: (0, 0))] * (2 * n),
        token,
        jax.ShapeDtypeStruct((t, d), BF16),
        4 * t * d * n * f,
        4 * t * n * f,
        name="by_input",
    )(h, dy, *dgs, *dus, *wgs, *wus)


def adamw_kernel(had, *refs):
    grads, refs = refs[:3], refs[3:]
    old, new = refs[:9], refs[9 + had :]
    for k in range(3):
        g = grads[k][0, 0].astype(F32)
        w, m, v = (old[k + 3 * which][0] for which in range(3))
        m = 0.9 * m + 0.1 * g
        v = 0.95 * v + 0.05 * g * g
        w = w.astype(F32)
        new[k][0] = (w - 0.02 * (m * lax.rsqrt(v + 1e-8) + 0.1 * w)).astype(BF16)
        new[k + 3][0] = m
        new[k + 6][0] = v


def adamw(grads, arrays, so_far, layer, start, group):
    n, _, rows, width = grads.shape
    part = width // group
    wide = pl.BlockSpec((1, rows, part), lambda c, i: (layer, 0, CHUNKS * i + c + start))
    tall = pl.BlockSpec((1, rows // group, width), lambda c, i: (layer, group * (c + start) + i, 0))
    blocks = [wide, wide, tall] * 3
    sums = [
        pl.BlockSpec((1, 1, rows, part), lambda c, i: (c, 1, 0, i)),
        pl.BlockSpec((1, 1, rows, part), lambda c, i: (c, 2, 0, i)),
        pl.BlockSpec((1, 1, rows // group, width), lambda c, i: (c, 0, i, 0)),
    ]
    had = len(so_far)
    return call(
        functools.partial(adamw_kernel, had),
        (n, group),
        sums + blocks + [pl.BlockSpec(memory_space=pl.ANY)] * had,
        blocks,
        [jax.ShapeDtypeStruct(a.shape, a.dtype) for a in arrays],
        20 * grads.size,
        22 * grads.size,
        aliases={3 + len(arrays) + k: k for k in range(had)},
        name="adamw",
    )(grads, grads, grads, *arrays, *so_far)


def solution(mesh):
    group = mesh.shape["dp"]

    def step(x, dy, *arrays):
        weights = arrays[:3]
        layers, rows, width = weights[0].shape
        h0, dy = x[0], dy[0]

        def summed(grads):
            _, n, _, rows, width = grads.shape
            mine = lax.psum_scatter(grads.reshape(group * n * 3 * rows, width), "dp", scatter_dimension=0, tiled=True)
            return mine.reshape(n, 3, rows, width)

        ident = iter(range(100))

        def beside(*pieces, when):
            gather = Gather([(which, layer, chunk, which == 2) for which, layer, chunk in pieces], group)
            return dict(gather=gather, when=when, ident=next(ident), sources=weights)

        wg, wu, wd = ([[None] * CHUNKS for _ in range(layers)] for _ in range(3))

        def keep(got, *pieces):
            for array, (which, layer, chunk) in zip(got, pieces, strict=True):
                (wg, wu, wd)[which][layer][chunk] = array

        pieces = (0, 0, 0), (1, 0, 0)
        extra = beside(*pieces, when=(1, 1))
        keep(fetch(extra["gather"], extra["ident"], weights), *pieces)
        plan = [
            [(0, 0, 1), (1, 0, 1)],
            [(0, 0, 2), (1, 0, 2), (2, 0, 0)],
            [(0, 0, 3), (1, 0, 3), (2, 0, 1)],
            [(2, 0, 2), (2, 0, 3)],
        ]
        ps, gates, ups, a0 = [], [], [], None
        for c in range(CHUNKS):
            got = gate_up(c == 0, h0 if c == 0 else a0, wg[0][c], wu[0][c], **beside(*plan[c], when=(5, 8)))
            if c == 0:
                a0, *got = got
            p, gate, up, *got = got
            keep(got, *plan[c])
            ps.append(p)
            gates.append(gate)
            ups.append(up)
        pieces = [(which, 1, 0) for which in range(3)]
        h1, a1, *got = down(ps, wd[0], h0, **beside(*pieces, when=(4, 6)))
        keep(got, *pieces)
        sums, qs, dgs, dus = [], [], [], []
        for c in range(CHUNKS):
            pieces = [(which, 1, c + 1) for which in range(3)] if c + 1 < CHUNKS else []
            q, dg, du, *got = hidden(a1, dy, wg[1][c], wu[1][c], wd[1][c], **(beside(*pieces, when=(5, 8)) if pieces else {}))
            keep(got, *pieces)
            qs.append(q)
            dgs.append(dg)
            dus.append(du)
            for start, stop in LAST_RANGES:
                if stop == c + 1:
                    sums.append((1, start, summed(by_weights(qs[start:stop], dgs[start:stop], dus[start:stop], dy, a1, group))))
        dh = by_input(h1, dy, dgs, dus, wg[1], wu[1])
        for c in range(CHUNKS):
            dg, du = hidden_back(dh, wd[0][c], gates[c], ups[c])
            sums.append((0, c, summed(by_weights([ps[c]], [dg], [du], dh, a0, group))))
        new = ()
        for layer, start, grads in sums:
            new = adamw(grads, arrays, new, layer, start, group)
        return tuple(new)

    states, cut = P(("rep", "dp"), None, None), P(None, "dp", None)
    return jax.shard_map(
        step,
        mesh=mesh,
        in_specs=(states, states) + (cut,) * 9,
        out_specs=(P("rep", "dp", None),) * 9,
        check_vma=False,
    )
```

time: 1250 us -> 1000 us (0.80)
  Pallas kernels: 0 us -> 968 us
  matrix products: 770 us -> 0 us
  waiting for transfers between devices: 347 us -> 9.71 us
  other arithmetic: 64.1 us -> 0 us
  local copies, waits for them, and re-layouts: 39.8 us -> 0 us
    pallas_call x0 -> x31, Pallas kernels: none -> 968 us  [the longest x9 376 us: call(): return run if gather is None else lambda *operands: run(*operands, *sources)]
    dot_general x15 -> x0, matrix products: 770 us -> none  [the longest x5 281 us: layer(): gate = jnp.dot(a, w['w_gate'], preferred_element_type=jnp.float32)]
    all_gather x6 -> x0, waiting for transfers between devices: 201 us -> none  [fetched(): lax.all_gather(w[number], 'dp', axis=0, tiled=True)]
    reduce_scatter x6 -> x8, waiting for transfers between devices: 143 us -> 9.28 us  [summed(): lax.psum_scatter(grads.reshape(group * n * 3 * rows, width), 'dp', scatte...]
    convert_element_type x3 -> x0, other arithmetic: 45.1 us -> none  [adamw(): return ((w - 0.02 * step).astype(jnp.bfloat16), m, v)]
    unnamed x18 -> x0, local copies, waits for them, and re-layouts: 25.6 us -> none
    slice x3 -> x0, local copies, waits for them, and re-layouts: 14.1 us -> none  [fetched(): w[number]]
    add_any x1 -> x0, other arithmetic: 13.9 us -> none  [normed(): wide = h.astype(jnp.float32)]
  transfers between devices with their start and end apart: 12 -> 8, of which waited for: 8 -> 1; matrix products, arithmetic and copies ran while one was open for 50% -> 0% of each run, Pallas kernels for 0% -> 68%
where the time goes in v1:
time: 1000 us; the launch traced here: 993 us
  Pallas kernels  968 us (97%)
  between operations  14.6 us (1%)
    pallas_call x9, Pallas kernels, call(): return run if gather is None else lambda *operands: run(*operands, *sources)  376 us
    pallas_call x8, Pallas kernels, by_weights(): call(functools.partial(by_weights_kernel, n, halves), (n * halves, steps)...  298 us
    pallas_call x4, Pallas kernels, hidden_back(): call(hidden_back_kernel, (t // tm,), [token, once((f, d), lambda i: (0, 0...  108 us
    pallas_call x1, Pallas kernels, by_input(): call(functools.partial(by_input_kernel, n), (t // tm,), [token, token] +...  89.9 us
    pallas_call x8, Pallas kernels, adamw(): call(functools.partial(adamw_kernel, had), (n, group), sums + blocks + [p...  59.2 us
    pallas_call x1, Pallas kernels, hidden(): call(hidden_kernel, (t // tm,), [token, token, whole((d, f)), whole((d, f...  36.8 us
  transfers between devices with their start and end apart: 8, of which 1 were waited for; matrix products, arithmetic and copies ran while one was open for 0% of the time, Pallas kernels for 68%

profile of v1, /device:TPU:112, one launch (start us, length us, event | category | flops | bytes accessed | tf_op | source)
XLA Modules:
  0.0 992.9 jit_solution(12983620278749609419)
XLA Ops:
  7.3 24.6 %fetch.1 = (bf16[1024,1024]{1,0:T(8,128)(2,1)}, bf16[1024,1024]{1,0:T(8,128)(2,1)}) custom-call(bf16[2,256,4096]{2,1,0:T(8,128)(2,1)} %refs_3_.23, bf16[2,256,4096]{2,1,0:T(8,128)(2,1)} %refs_4_.23, bf16[2,1024,1024]{2,1,0:T(8,128)(2,1)} %refs_5_.29), custom_call_target="tpu_custom_call" | custom-call | flops 1000000000 | bytes 10000000 | tf_op jit(solution)/shard_map/fetch/pallas_call | solution.py:81
  31.9 30.6 %gate_up.4 = (bf16[4096,1024]{1,0:T(8,128)(2,1)}, bf16[4096,1024]{1,0:T(8,128)(2,1)}, f32[4096,1024]{1,0:T(8,128)}, f32[4096,1024]{1,0:T(8,128)}, bf16[1024,1024...) custom-call(bf16[4096,1024]{1,0:T(8,128)(2,1)} %bitcast.50, bf16[1024,1024]{1,0:T(8,128)(2,1)} %get-tuple-element.131.refs_1_, ...), custom_call_target="tpu_custom_call" | custom-call | flops 17179869184 | bytes 41943040 | tf_op jit(solution)/shard_map/gate_up/pallas_call | solution.py:81
  62.5 36.7 %gate_up.5 = (bf16[4096,1024]{1,0:T(8,128)(2,1)}, f32[4096,1024]{1,0:T(8,128)}, f32[4096,1024]{1,0:T(8,128)}, bf16[1024,1024]{1,0:T(8,128)(2,1)}, bf16[1024,1024...) custom-call(bf16[4096,1024]{1,0:T(8,128)(2,1)} %get-tuple-element.134.refs_0_.a, bf16[1024,1024]{1,0:T(8,128)(2,1)} %get-tuple-element.135.refs_1_, ...), custom_call_target="tpu_custom_call" | custom-call | flops 17179869184 | bytes 41943040 | tf_op jit(solution)/shard_map/gate_up/pallas_call | solution.py:81
  99.1 36.5 %gate_up.6 = (bf16[4096,1024]{1,0:T(8,128)(2,1)}, f32[4096,1024]{1,0:T(8,128)}, f32[4096,1024]{1,0:T(8,128)}, bf16[1024,1024]{1,0:T(8,128)(2,1)}, bf16[1024,1024...) custom-call(bf16[4096,1024]{1,0:T(8,128)(2,1)} %get-tuple-element.134.refs_0_.a, bf16[1024,1024]{1,0:T(8,128)(2,1)} %get-tuple-element.138.refs_1_, ...), custom_call_target="tpu_custom_call" | custom-call | flops 17179869184 | bytes 41943040 | tf_op jit(solution)/shard_map/gate_up/pallas_call | solution.py:81
  135.7 29.7 %gate_up.7 = (bf16[4096,1024]{1,0:T(8,128)(2,1)}, f32[4096,1024]{1,0:T(8,128)}, f32[4096,1024]{1,0:T(8,128)}, bf16[1024,1024]{1,0:T(8,128)(2,1)}, bf16[1024,1024]{1,0:T(8,128)(2,1)}) custom-call(bf16[4096,1024]{1,0:T(8,128)(2,1)} %get-tuple-element.134.refs_0_.a, bf16[1024,1024]{1,0:T(8,128)(2,1)} %get-tuple-element.141.refs_1_, ...), custom_call_target="tpu_custom_call" | custom-call | flops 17179869184 | bytes 41943040 | tf_op jit(solution)/shard_map/gate_up/pallas_call | solution.py:81
  165.4 50.8 %down.1 = (bf16[4096,1024]{1,0:T(8,128)(2,1)}, bf16[4096,1024]{1,0:T(8,128)(2,1)}, bf16[1024,1024]{1,0:T(8,128)(2,1)}, bf16[1024,1024]{1,0:T(8,128)(2,1)}, bf16[1024,1024]{1,0:T(8,128)(2,1)}) custom-call(bf16[4096,1024]{1,0:T(8,128)(2,1)} %bitcast.51, bf16[4096,1024]{1,0:T(8,128)(2,1)} %get-tuple-element.133.refs_1_.refs_0_, ...), custom_call_target="tpu_custom_call" | custom-call | flops 34359738368 | bytes 33554432 | tf_op jit(solution)/shard_map/down/pallas_call | solution.py:81
  216.2 42.3 %hidden.4 = (bf16[4096,1024]{1,0:T(8,128)(2,1)}, bf16[4096,1024]{1,0:T(8,128)(2,1)}, bf16[4096,1024]{1,0:T(8,128)(2,1)}, bf16[1024,1024]{1,0:T(8,128)(2,1)}, bf1...) custom-call(bf16[4096,1024]{1,0:T(8,128)(2,1)} %get-tuple-element.149.refs_0_.a, bf16[4096,1024]{1,0:T(8,128)(2,1)} %bitcast.52, ...), custom_call_target="tpu_custom_call" | custom-call | flops 25769803776 | bytes 25165824 | tf_op jit(solution)/shard_map/hidden/pallas_call | solution.py:81
  258.6 37.3 %by_weights.15 = bf16[4,1,3,256,1024]{4,3,2,1,0:T(8,128)(2,1)} custom-call(bf16[4096,1024]{1,0:T(8,128)(2,1)} %bitcast.53, bf16[4096,1024]{1,0:T(8,128)(2,1)} %get-tuple-element.149.refs_0_.a, bf16[4096,1024]{1,0:T(8,128)(2,1)} %get-tuple-element.189.refs_0_, bf16[4096,1024]{1,0:T(8,128)(2,1)} %get-tuple-element.153.refs_0_.refs_1_, ...), custom_call_target="tpu_custom_call" | custom-call | flops 25769803776 | bytes 41943040 | tf_op jit(solution)/shard_map/by_weights/pallas_call | solution.py:388
  296.0 62.2 %hidden.5 = (bf16[4096,1024]{1,0:T(8,128)(2,1)}, bf16[4096,1024]{1,0:T(8,128)(2,1)}, bf16[4096,1024]{1,0:T(8,128)(2,1)}, bf16[1024,1024]{1,0:T(8,128)(2,1)}, bf1...) custom-call(bf16[4096,1024]{1,0:T(8,128)(2,1)} %get-tuple-element.149.refs_0_.a, bf16[4096,1024]{1,0:T(8,128)(2,1)} %bitcast.54, ...), custom_call_target="tpu_custom_call" | custom-call | flops 25769803776 | bytes 25165824 | tf_op jit(solution)/shard_map/hidden/pallas_call | solution.py:81
  358.3 37.2 %by_weights.14 = bf16[4,1,3,256,1024]{4,3,2,1,0:T(8,128)(2,1)} custom-call(bf16[4096,1024]{1,0:T(8,128)(2,1)} %bitcast.55, bf16[4096,1024]{1,0:T(8,128)(2,1)} %get-tuple-element.149.refs_0_.a, bf16[4096,1024]{1,0:T(8,128)(2,1)} %get-tuple-element.188.refs_0_, bf16[4096,1024]{1,0:T(8,128)(2,1)} %get-tuple-element.157.refs_1_, ...), custom_call_target="tpu_custom_call" | custom-call | flops 25769803776 | bytes 41943040 | tf_op jit(solution)/shard_map/by_weights/pallas_call | solution.py:388
  395.6 62.4 %hidden.6 = (bf16[4096,1024]{1,0:T(8,128)(2,1)}, bf16[4096,1024]{1,0:T(8,128)(2,1)}, bf16[4096,1024]{1,0:T(8,128)(2,1)}, bf16[1024,1024]{1,0:T(8,128)(2,1)}, bf1...) custom-call(bf16[4096,1024]{1,0:T(8,128)(2,1)} %get-tuple-element.149.refs_0_.a, bf16[4096,1024]{1,0:T(8,128)(2,1)} %bitcast.56, ...), custom_call_target="tpu_custom_call" | custom-call | flops 25769803776 | bytes 25165824 | tf_op jit(solution)/shard_map/hidden/pallas_call | solution.py:81
  458.0 37.2 %by_weights.13 = bf16[4,1,3,256,1024]{4,3,2,1,0:T(8,128)(2,1)} custom-call(bf16[4096,1024]{1,0:T(8,128)(2,1)} %bitcast.57, bf16[4096,1024]{1,0:T(8,128)(2,1)} %get-tuple-element.149.refs_0_.a, bf16[4096,1024]{1,0:T(8,128)(2,1)} %get-tuple-element.187.refs_0_, bf16[4096,1024]{1,0:T(8,128)(2,1)} %get-tuple-element.161.refs_2_.refs_1_, ...), custom_call_target="tpu_custom_call" | custom-call | flops 25769803776 | bytes 41943040 | tf_op jit(solution)/shard_map/by_weights/pallas_call | solution.py:388
  495.3 36.8 %hidden.7 = (bf16[4096,1024]{1,0:T(8,128)(2,1)}, bf16[4096,1024]{1,0:T(8,128)(2,1)}, bf16[4096,1024]{1,0:T(8,128)(2,1)}) custom-call(bf16[4096,1024]{1,0:T(8,128)(2,1)} %get-tuple-element.149.refs_0_.a, bf16[4096,1024]{1,0:T(8,128)(2,1)} %bitcast.58, bf16[1024,1024]{1,0:T(8,128)(2,1)} %get-tuple-element.162.wg.refs_11_, ...), custom_call_target="tpu_custom_call" | custom-call | flops 25769803776 | bytes 25165824 | tf_op jit(solution)/shard_map/hidden/pallas_call | solution.py:301
  532.1 37.3 %by_weights.12 = bf16[4,1,3,256,1024]{4,3,2,1,0:T(8,128)(2,1)} custom-call(bf16[4096,1024]{1,0:T(8,128)(2,1)} %bitcast.59, bf16[4096,1024]{1,0:T(8,128)(2,1)} %get-tuple-element.149.refs_0_.a, bf16[4096,1024]{1,0:T(8,128)(2,1)} %get-tuple-element.186.refs_0_, bf16[4096,1024]{1,0:T(8,128)(2,1)} %get-tuple-element.165.refs_3_.refs_1_, ...), custom_call_target="tpu_custom_call" | custom-call | flops 25769803776 | bytes 41943040 | tf_op jit(solution)/shard_map/by_weights/pallas_call | solution.py:388
  569.6 89.9 %by_input.1.dh.dy = bf16[4096,1024]{1,0:T(8,128)(2,1)} custom-call(bf16[4096,1024]{1,0:T(8,128)(2,1)} %get-tuple-element.148.h, bf16[4096,1024]{1,0:T(8,128)(2,1)} %bitcast.60, bf16[4096,1024]{1,0:T(8,128)(2,1)} %get-tuple-element.153.refs_0_.refs_1_, bf16[4096,1024]{1,0:T(8,128)(2,1)} %get-tuple-element.157.refs_1_, ...), custom_call_target="tpu_custom_call" | custom-call | flops 68719476736 | bytes 67108864 | tf_op jit(solution)/shard_map/by_input/pallas_call | solution.py:424
  659.5 26.8 %hidden_back.7 = (bf16[4096,1024]{1,0:T(8,128)(2,1)}, bf16[4096,1024]{1,0:T(8,128)(2,1)}) custom-call(bf16[4096,1024]{1,0:T(8,128)(2,1)} %by_input.1.dh.dy, bf16[1024,1024]{1,0:T(8,128)(2,1)} %get-tuple-element.144.refs_5_.wd, f32[4096,1024]{1,0:T(8,128)} %get-tuple-element.182.gate, f32[4096,1024]{1,0:T(8,128)} %get-tuple-element.183.up), custom_call_target="tpu_custom_call" | custom-call | flops 8589934592 | bytes 50331648 | tf_op jit(solution)/shard_map/hidden_back/pallas_call | solution.py:330
  686.2 37.5 %by_weights.11 = bf16[4,1,3,256,1024]{4,3,2,1,0:T(8,128)(2,1)} custom-call(bf16[4096,1024]{1,0:T(8,128)(2,1)} %by_input.1.dh.dy, bf16[4096,1024]{1,0:T(8,128)(2,1)} %get-tuple-element.134.refs_0_.a, bf16[4096,1024]{1,0:T(8,128)(2,1)} %get-tuple-element.133.refs_1_.refs_0_, bf16[4096,1024]{1,0:T(8,128)(2,1)} %get-tuple-element.184.refs_1_, ...), custom_call_target="tpu_custom_call" | custom-call | flops 25769803776 | bytes 41943040 | tf_op jit(solution)/shard_map/by_weights/pallas_call | solution.py:388
  723.9 27.2 %hidden_back.6 = (bf16[4096,1024]{1,0:T(8,128)(2,1)}, bf16[4096,1024]{1,0:T(8,128)(2,1)}) custom-call(bf16[4096,1024]{1,0:T(8,128)(2,1)} %by_input.1.dh.dy, bf16[1024,1024]{1,0:T(8,128)(2,1)} %get-tuple-element.145.refs_6_.wd, f32[4096,1024]{1,0:T(8,128)} %get-tuple-element.178.gate, f32[4096,1024]{1,0:T(8,128)} %get-tuple-element.179.up), custom_call_target="tpu_custom_call" | custom-call | flops 8589934592 | bytes 50331648 | tf_op jit(solution)/shard_map/hidden_back/pallas_call | solution.py:330
  751.1 37.3 %by_weights.10 = bf16[4,1,3,256,1024]{4,3,2,1,0:T(8,128)(2,1)} custom-call(bf16[4096,1024]{1,0:T(8,128)(2,1)} %by_input.1.dh.dy, bf16[4096,1024]{1,0:T(8,128)(2,1)} %get-tuple-element.134.refs_0_.a, bf16[4096,1024]{1,0:T(8,128)(2,1)} %get-tuple-element.137.refs_2_.refs_0_, bf16[4096,1024]{1,0:T(8,128)(2,1)} %get-tuple-element.180.refs_1_, ...), custom_call_target="tpu_custom_call" | custom-call | flops 25769803776 | bytes 41943040 | tf_op jit(solution)/shard_map/by_weights/pallas_call | solution.py:388
  788.6 27.0 %hidden_back.5 = (bf16[4096,1024]{1,0:T(8,128)(2,1)}, bf16[4096,1024]{1,0:T(8,128)(2,1)}) custom-call(bf16[4096,1024]{1,0:T(8,128)(2,1)} %by_input.1.dh.dy, bf16[1024,1024]{1,0:T(8,128)(2,1)} %get-tuple-element.146.refs_7_.wd, f32[4096,1024]{1,0:T(8,128)} %get-tuple-element.174.gate, f32[4096,1024]{1,0:T(8,128)} %get-tuple-element.175.up), custom_call_target="tpu_custom_call" | custom-call | flops 8589934592 | bytes 50331648 | tf_op jit(solution)/shard_map/hidden_back/pallas_call | solution.py:330
  815.5 37.2 %by_weights.9 = bf16[4,1,3,256,1024]{4,3,2,1,0:T(8,128)(2,1)} custom-call(bf16[4096,1024]{1,0:T(8,128)(2,1)} %by_input.1.dh.dy, bf16[4096,1024]{1,0:T(8,128)(2,1)} %get-tuple-element.134.refs_0_.a, bf16[4096,1024]{1,0:T(8,128)(2,1)} %get-tuple-element.140.refs_3_.refs_0_, bf16[4096,1024]{1,0:T(8,128)(2,1)} %get-tuple-element.176.refs_1_, ...), custom_call_target="tpu_custom_call" | custom-call | flops 25769803776 | bytes 41943040 | tf_op jit(solution)/shard_map/by_weights/pallas_call | solution.py:388
  852.8 27.0 %hidden_back.4 = (bf16[4096,1024]{1,0:T(8,128)(2,1)}, bf16[4096,1024]{1,0:T(8,128)(2,1)}) custom-call(bf16[4096,1024]{1,0:T(8,128)(2,1)} %by_input.1.dh.dy, bf16[1024,1024]{1,0:T(8,128)(2,1)} %get-tuple-element.147.refs_8_.wd, f32[4096,1024]{1,0:T(8,128)} %get-tuple-element.170.gate, f32[4096,1024]{1,0:T(8,128)} %get-tuple-element.171.up), custom_call_target="tpu_custom_call" | custom-call | flops 8589934592 | bytes 50331648 | tf_op jit(solution)/shard_map/hidden_back/pallas_call | solution.py:330
  879.8 37.3 %by_weights.8 = bf16[4,1,3,256,1024]{4,3,2,1,0:T(8,128)(2,1)} custom-call(bf16[4096,1024]{1,0:T(8,128)(2,1)} %by_input.1.dh.dy, bf16[4096,1024]{1,0:T(8,128)(2,1)} %get-tuple-element.134.refs_0_.a, bf16[4096,1024]{1,0:T(8,128)(2,1)} %get-tuple-element.143.refs_4_.refs_0_, bf16[4096,1024]{1,0:T(8,128)(2,1)} %get-tuple-element.172.refs_1_, ...), custom_call_target="tpu_custom_call" | custom-call | flops 25769803776 | bytes 41943040 | tf_op jit(solution)/shard_map/by_weights/pallas_call | solution.py:388
  969.3 9.1 reduce-scatter.9.cloned.1.call-done
  (31 shorter events, 60.3 us)
Async XLA Ops:
  7.2 910.0 %reduce-scatter.23.cloned.1.call-start = ((), (), s32[]{:S(2)}) async-start(), calls=%async_computation.15 | async-start | bytes 7864320 | tf_op jit(solution)/shard_map/reduce_scatter | solution.py:485
  296.0 628.6 %reduce-scatter.21.cloned.1.call-start = ((), (), s32[]{:S(2)}) async-start(), calls=%async_computation.14 | async-start | bytes 7864320 | tf_op jit(solution)/shard_map/reduce_scatter | solution.py:485
  395.5 536.5 %reduce-scatter.19.cloned.1.call-start = ((), (), s32[]{:S(2)}) async-start(), calls=%async_computation.13 | async-start | bytes 7864320 | tf_op jit(solution)/shard_map/reduce_scatter | solution.py:485
  495.3 444.2 %reduce-scatter.17.cloned.1.call-start = ((), (), s32[]{:S(2)}) async-start(), calls=%async_computation.12 | async-start | bytes 7864320 | tf_op jit(solution)/shard_map/reduce_scatter | solution.py:485
  569.5 377.5 %reduce-scatter.15.cloned.1.call-start = ((), (), s32[]{:S(2)}) async-start(), calls=%async_computation.11 | async-start | bytes 7864320 | tf_op jit(solution)/shard_map/reduce_scatter | solution.py:485
  723.8 230.6 %reduce-scatter.13.cloned.1.call-start = ((), (), s32[]{:S(2)}) async-start(), calls=%async_computation.10 | async-start | bytes 7864320 | tf_op jit(solution)/shard_map/reduce_scatter | solution.py:485
  788.5 173.3 %reduce-scatter.11.cloned.1.call-start = ((), (), s32[]{:S(2)}) async-start(), calls=%async_computation.9 | async-start | bytes 7864320 | tf_op jit(solution)/shard_map/reduce_scatter | solution.py:485
  852.8 125.6 %reduce-scatter.9.cloned.1.call-start = ((), (), s32[]{:S(2)}) async-start(), calls=%async_computation.8 | async-start | bytes 7864320 | tf_op jit(solution)/shard_map/reduce_scatter | solution.py:485
Sparse Core Ops, SparseCore 0:
  296.1 85.3 reduce-scatter.22
  395.7 85.5 reduce-scatter.20
  495.4 61.0 reduce-scatter.18
  569.6 61.0 reduce-scatter.16
  723.9 61.0 reduce-scatter.14
  788.6 61.0 reduce-scatter.12
  852.9 61.0 reduce-scatter.10
  917.3 61.0 reduce-scatter.8

commit v2 on v1

--- a/solution.py
+++ b/solution.py
@@ -10,7 +10,6 @@
 F32, BF16 = jnp.float32, jnp.bfloat16
 VMEM_LIMIT = 61 * 2**20
 CHUNKS = 4
-LAST_RANGES = ((0, 1), (1, 2), (2, 3), (3, 4))
 
 
 def dot(a, b, over_a, over_b):
@@ -311,37 +310,64 @@
     )(a, dy, wg, wu, wd)
 
 
-def hidden_back_kernel(dh, wd, gate, up, dg, du):
-    half = wd.shape[0] // 2
+def first_kernel(dh, a, wd, gate, up, p, out, dg, du, acc_d, acc_g, acc_u):
+    i, last = pl.program_id(1), pl.num_programs(1) - 1
+    width = wd.shape[0]
+    half = width // 2
     for part in range(2):
         cols = pl.ds(part * half, half)
         dp = rounded(dot(dh[...], wd[cols, :], 1, 1))
         _, by_g, by_u = hidden_gradients(gate[:, cols], up[:, cols], dp)
         dg[:, cols] = by_g.astype(BF16)
         du[:, cols] = by_u.astype(BF16)
-
-
-def hidden_back(dh, wd, gate, up):
-    t, d = dh.shape
+    terms = dot(p[...], dh[...], 0, 0), dot(a[...], dg[...], 0, 0), dot(a[...], du[...], 0, 0)
+    accs = acc_d, acc_g, acc_u
+
+    @pl.when(i == 0)
+    def _():
+        for acc, term in zip(accs, terms):
+            acc[...] = term
+
+    @pl.when(i > 0)
+    def _():
+        for acc, term in zip(accs, terms):
+            acc[...] += term
+
+    group, rows = out.shape[0], out.shape[3]
+    halves = out.shape[4] // width
+    part = group // halves
+    for h in range(halves):
+
+        @pl.when((i == last) & (pl.program_id(0) == h))
+        def _():
+            out[h * part : (h + 1) * part, 0, 0] = acc_d[...].astype(BF16).reshape(part, rows, out.shape[4])
+            out[:, 0, 1, :, h * width : (h + 1) * width] = acc_g[...].astype(BF16).reshape(group, rows, width)
+            out[:, 0, 2, :, h * width : (h + 1) * width] = acc_u[...].astype(BF16).reshape(group, rows, width)
+
+
+def first_back(dh, a, wd, gate, up, p, group):
+    t, d = a.shape
     f = wd.shape[0]
-    tm = min(t, 512)
-    token = pl.BlockSpec((tm, d), lambda i: (i, 0))
-    tile = pl.BlockSpec((tm, f), lambda i: (i, 0))
-    return call(
-        hidden_back_kernel,
-        (t // tm,),
-        [token, once((f, d), lambda i: (0, 0)), tile, tile],
-        [tile] * 2,
-        [jax.ShapeDtypeStruct((t, f), BF16)] * 2,
-        2 * t * d * f,
-        12 * t * f,
-        name="hidden_back",
-    )(dh, wd, gate, up)
+    halves, tm = 2, min(t, 1024)
+    width = f // halves
+    token = pl.BlockSpec((tm, d), lambda j, i: (i, 0))
+    tile = pl.BlockSpec((tm, width), lambda j, i: (i, j))
+    return call(
+        first_kernel,
+        (halves, t // tm),
+        [token, token, pl.BlockSpec((width, d), lambda j, i: (j, 0)), tile, tile, tile],
+        pl.BlockSpec((group, 1, 3, d // group, f), lambda j, i: (0, 0, 0, 0, 0)),
+        jax.ShapeDtypeStruct((group, 1, 3, d // group, f), BF16),
+        8 * t * d * f,
+        10 * t * f,
+        [pltpu.VMEM((tm, width), BF16)] * 2 + [pltpu.VMEM((width, d), F32)] + [pltpu.VMEM((d, width), F32)] * 2,
+        name="first_back",
+    )(dh, a, wd, gate, up, p)
 
 
 def by_weights_kernel(n, halves, dy, a, *refs):
     ps, dgs, dus = (refs[k * n : k * n + n] for k in range(3))
-    out, acc_d, acc_g, acc_u = refs[3 * n :]
+    _, out, acc_d, acc_g, acc_u = refs[3 * n :]
     chunk, i = pl.program_id(0) // halves, pl.program_id(1)
     half = lax.rem(pl.program_id(0), halves)
     group, rows = out.shape[0], out.shape[3]
@@ -370,7 +396,7 @@
                         out[:, 0, 2, :, pl.ds(h * width, width)] = by_u.reshape(group, rows, width)
 
 
-def by_weights(ps, dgs, dus, dy, a, group):
+def by_weights(ps, dgs, dus, dy, a, group, after):
     t, d = a.shape
     n, f = len(ps), ps[0].shape[1]
     halves, steps = 2, 2
@@ -388,14 +414,14 @@
     return call(
         functools.partial(by_weights_kernel, n, halves),
         (n * halves, steps),
-        [token, token] + [tile(c) for c in range(n)] * 3,
+        [token, token] + [tile(c) for c in range(n)] * 3 + [ANY],
         pl.BlockSpec((group, 1, 3, d // group, f), lambda j, i: (0, j // halves, 0, 0, 0)),
         jax.ShapeDtypeStruct((group, n, 3, d // group, f), BF16),
         6 * t * d * f * n,
         10 * t * f * n,
         [pltpu.VMEM((width, d), F32)] + [pltpu.VMEM((d, width), F32)] * 2,
         name="by_weights",
-    )(dy, a, *ps, *dgs, *dus)
+    )(dy, a, *ps, *dgs, *dus, after)
 
 
 def by_input_kernel(n, h, dy, *refs):
@@ -527,13 +553,11 @@
             qs.append(q)
             dgs.append(dg)
             dus.append(du)
-            for start, stop in LAST_RANGES:
-                if stop == c + 1:
-                    sums.append((1, start, summed(by_weights(qs[start:stop], dgs[start:stop], dus[start:stop], dy, a1, group))))
+        for c in range(CHUNKS):
+            sums.append((1, c, summed(by_weights([qs[c]], [dgs[c]], [dus[c]], dy, a1, group, qs[CHUNKS - 2]))))
         dh = by_input(h1, dy, dgs, dus, wg[1], wu[1])
         for c in range(CHUNKS):
-            dg, du = hidden_back(dh, wd[0][c], gates[c], ups[c])
-            sums.append((0, c, summed(by_weights([ps[c]], [dg], [du], dh, a0, group))))
+            sums.append((0, c, summed(first_back(dh, a0, wd[0][c], gates[c], ups[c], ps[c], group))))
         new = ()
         for layer, start, grads in sums:
             new = adamw(grads, arrays, new, layer, start, group)

time: 1000 us -> 942 us (0.942)
  Pallas kernels: 968 us -> 875 us
  waiting for transfers between devices: 9.71 us -> 42 us
    pallas_call x8 -> x4, Pallas kernels: 298 us -> 150 us  [by_weights(): call(functools.partial(by_weights_kernel, n, halves), (n * halves, steps)...]
    pallas_call x4, Pallas kernels: 108 us -> 203 us  [first_back(): call(first_kernel, (halves, t // tm), [token, token, pl.BlockSpec((width,...]
    pallas_call x9, Pallas kernels: 376 us -> 336 us  [call(): return run if gather is None else lambda *operands: run(*operands, *sources)]
    reduce_scatter x8, waiting for transfers between devices: 9.28 us -> 41.6 us  [summed(): lax.psum_scatter(grads.reshape(group * n * 3 * rows, width), 'dp', scatte...]
  transfers between devices with their start and end apart: 8 -> 8, of which waited for: 1 -> 1; matrix products, arithmetic and copies ran while one was open for 0% -> 0% of each run, Pallas kernels for 68% -> 53%
where the time goes in v2:
time: 942 us; the launch traced here: 933 us
  Pallas kernels  875 us (93%)
  waiting for transfers between devices  42 us (4%)
  between operations  14.8 us (2%)
    pallas_call x9, Pallas kernels, call(): return run if gather is None else lambda *operands: run(*operands, *sources)  336 us
    pallas_call x4, Pallas kernels, first_back(): call(first_kernel, (halves, t // tm), [token, token, pl.BlockSpec((width,...  203 us
    pallas_call x4, Pallas kernels, by_weights(): call(functools.partial(by_weights_kernel, n, halves), (n * halves, steps)...  150 us
    pallas_call x1, Pallas kernels, by_input(): call(functools.partial(by_input_kernel, n), (t // tm,), [token, token] +...  90.1 us
    pallas_call x8, Pallas kernels, adamw(): call(functools.partial(adamw_kernel, had), (n, group), sums + blocks + [p...  59.2 us
    reduce_scatter x8, waiting for transfers between devices, summed(): lax.psum_scatter(grads.reshape(group * n * 3 * rows, width), 'dp', scatte...  41.6 us
    pallas_call x1, Pallas kernels, hidden(): call(hidden_kernel, (t // tm,), [token, token, whole((d, f)), whole((d, f...  36.6 us
  transfers between devices with their start and end apart: 8, of which 1 were waited for; matrix products, arithmetic and copies ran while one was open for 0% of the time, Pallas kernels for 53%

profile of v2, /device:TPU:112, one launch (start us, length us, event | category | flops | bytes accessed | tf_op | source)
XLA Modules:
  0.0 932.8 jit_solution(4370009256619252766)
XLA Ops:
  7.3 24.6 %fetch.1 = (bf16[1024,1024]{1,0:T(8,128)(2,1)}, bf16[1024,1024]{1,0:T(8,128)(2,1)}) custom-call(bf16[2,256,4096]{2,1,0:T(8,128)(2,1)} %refs_3_.23, bf16[2,256,4096]{2,1,0:T(8,128)(2,1)} %refs_4_.23, bf16[2,1024,1024]{2,1,0:T(8,128)(2,1)} %refs_5_.29), custom_call_target="tpu_custom_call" | custom-call | flops 1000000000 | bytes 10000000 | tf_op jit(solution)/shard_map/fetch/pallas_call | solution.py:80
  31.9 30.7 %gate_up.4 = (bf16[4096,1024]{1,0:T(8,128)(2,1)}, bf16[4096,1024]{1,0:T(8,128)(2,1)}, f32[4096,1024]{1,0:T(8,128)}, f32[4096,1024]{1,0:T(8,128)}, bf16[1024,1024...) custom-call(bf16[4096,1024]{1,0:T(8,128)(2,1)} %bitcast.50, bf16[1024,1024]{1,0:T(8,128)(2,1)} %get-tuple-element.123.refs_1_, ...), custom_call_target="tpu_custom_call" | custom-call | flops 17179869184 | bytes 41943040 | tf_op jit(solution)/shard_map/gate_up/pallas_call | solution.py:80
  62.6 36.5 %gate_up.5 = (bf16[4096,1024]{1,0:T(8,128)(2,1)}, f32[4096,1024]{1,0:T(8,128)}, f32[4096,1024]{1,0:T(8,128)}, bf16[1024,1024]{1,0:T(8,128)(2,1)}, bf16[1024,1024...) custom-call(bf16[4096,1024]{1,0:T(8,128)(2,1)} %get-tuple-element.126.refs_0_.a, bf16[1024,1024]{1,0:T(8,128)(2,1)} %get-tuple-element.127.refs_1_, ...), custom_call_target="tpu_custom_call" | custom-call | flops 17179869184 | bytes 41943040 | tf_op jit(solution)/shard_map/gate_up/pallas_call | solution.py:80
  99.1 36.6 %gate_up.6 = (bf16[4096,1024]{1,0:T(8,128)(2,1)}, f32[4096,1024]{1,0:T(8,128)}, f32[4096,1024]{1,0:T(8,128)}, bf16[1024,1024]{1,0:T(8,128)(2,1)}, bf16[1024,1024...) custom-call(bf16[4096,1024]{1,0:T(8,128)(2,1)} %get-tuple-element.126.refs_0_.a, bf16[1024,1024]{1,0:T(8,128)(2,1)} %get-tuple-element.130.refs_1_, ...), custom_call_target="tpu_custom_call" | custom-call | flops 17179869184 | bytes 41943040 | tf_op jit(solution)/shard_map/gate_up/pallas_call | solution.py:80
  135.7 29.8 %gate_up.7 = (bf16[4096,1024]{1,0:T(8,128)(2,1)}, f32[4096,1024]{1,0:T(8,128)}, f32[4096,1024]{1,0:T(8,128)}, bf16[1024,1024]{1,0:T(8,128)(2,1)}, bf16[1024,1024]{1,0:T(8,128)(2,1)}) custom-call(bf16[4096,1024]{1,0:T(8,128)(2,1)} %get-tuple-element.126.refs_0_.a, bf16[1024,1024]{1,0:T(8,128)(2,1)} %get-tuple-element.133.refs_1_, ...), custom_call_target="tpu_custom_call" | custom-call | flops 17179869184 | bytes 41943040 | tf_op jit(solution)/shard_map/gate_up/pallas_call | solution.py:80
  165.4 50.8 %down.1 = (bf16[4096,1024]{1,0:T(8,128)(2,1)}, bf16[4096,1024]{1,0:T(8,128)(2,1)}, bf16[1024,1024]{1,0:T(8,128)(2,1)}, bf16[1024,1024]{1,0:T(8,128)(2,1)}, bf16[1024,1024]{1,0:T(8,128)(2,1)}) custom-call(bf16[4096,1024]{1,0:T(8,128)(2,1)} %bitcast.51, bf16[4096,1024]{1,0:T(8,128)(2,1)} %get-tuple-element.125.refs_1_.p, ...), custom_call_target="tpu_custom_call" | custom-call | flops 34359738368 | bytes 33554432 | tf_op jit(solution)/shard_map/down/pallas_call | solution.py:80
  216.3 42.4 %hidden.4 = (bf16[4096,1024]{1,0:T(8,128)(2,1)}, bf16[4096,1024]{1,0:T(8,128)(2,1)}, bf16[4096,1024]{1,0:T(8,128)(2,1)}, bf16[1024,1024]{1,0:T(8,128)(2,1)}, bf1...) custom-call(bf16[4096,1024]{1,0:T(8,128)(2,1)} %get-tuple-element.141.refs_0_.a, bf16[4096,1024]{1,0:T(8,128)(2,1)} %bitcast.52, ...), custom_call_target="tpu_custom_call" | custom-call | flops 25769803776 | bytes 25165824 | tf_op jit(solution)/shard_map/hidden/pallas_call | solution.py:80
  258.7 42.5 %hidden.5 = (bf16[4096,1024]{1,0:T(8,128)(2,1)}, bf16[4096,1024]{1,0:T(8,128)(2,1)}, bf16[4096,1024]{1,0:T(8,128)(2,1)}, bf16[1024,1024]{1,0:T(8,128)(2,1)}, bf1...) custom-call(bf16[4096,1024]{1,0:T(8,128)(2,1)} %get-tuple-element.141.refs_0_.a, bf16[4096,1024]{1,0:T(8,128)(2,1)} %bitcast.53, ...), custom_call_target="tpu_custom_call" | custom-call | flops 25769803776 | bytes 25165824 | tf_op jit(solution)/shard_map/hidden/pallas_call | solution.py:80
  301.2 42.4 %hidden.6 = (bf16[4096,1024]{1,0:T(8,128)(2,1)}, bf16[4096,1024]{1,0:T(8,128)(2,1)}, bf16[4096,1024]{1,0:T(8,128)(2,1)}, bf16[1024,1024]{1,0:T(8,128)(2,1)}, bf1...) custom-call(bf16[4096,1024]{1,0:T(8,128)(2,1)} %get-tuple-element.141.refs_0_.a, bf16[4096,1024]{1,0:T(8,128)(2,1)} %bitcast.54, ...), custom_call_target="tpu_custom_call" | custom-call | flops 25769803776 | bytes 25165824 | tf_op jit(solution)/shard_map/hidden/pallas_call | solution.py:80
  343.7 37.8 %by_weights.7 = bf16[4,1,3,256,1024]{4,3,2,1,0:T(8,128)(2,1)} custom-call(bf16[4096,1024]{1,0:T(8,128)(2,1)} %bitcast.55, bf16[4096,1024]{1,0:T(8,128)(2,1)} %get-tuple-element.141.refs_0_.a, bf16[4096,1024]{1,0:T(8,128)(2,1)} %get-tuple-element.173.refs_0_, bf16[4096,1024]{1,0:T(8,128)(2,1)} %get-tuple-element.145.refs_0_.refs_1_, ...), custom_call_target="tpu_custom_call" | custom-call | flops 25769803776 | bytes 41943040 | tf_op jit(solution)/shard_map/by_weights/pallas_call | solution.py:414
  381.6 37.2 %by_weights.6 = bf16[4,1,3,256,1024]{4,3,2,1,0:T(8,128)(2,1)} custom-call(bf16[4096,1024]{1,0:T(8,128)(2,1)} %bitcast.56, bf16[4096,1024]{1,0:T(8,128)(2,1)} %get-tuple-element.141.refs_0_.a, bf16[4096,1024]{1,0:T(8,128)(2,1)} %get-tuple-element.172.refs_0_, bf16[4096,1024]{1,0:T(8,128)(2,1)} %get-tuple-element.149.refs_1_, ...), custom_call_target="tpu_custom_call" | custom-call | flops 25769803776 | bytes 41943040 | tf_op jit(solution)/shard_map/by_weights/pallas_call | solution.py:414
  418.9 37.5 %by_weights.5 = bf16[4,1,3,256,1024]{4,3,2,1,0:T(8,128)(2,1)} custom-call(bf16[4096,1024]{1,0:T(8,128)(2,1)} %bitcast.57, bf16[4096,1024]{1,0:T(8,128)(2,1)} %get-tuple-element.141.refs_0_.a, bf16[4096,1024]{1,0:T(8,128)(2,1)} %get-tuple-element.171.refs_3_.refs_0_, bf16[4096,1024]{1,0:T(8,128)(2,1)} %get-tuple-element.153.refs_2_.refs_1_, ...), custom_call_target="tpu_custom_call" | custom-call | flops 25769803776 | bytes 41943040 | tf_op jit(solution)/shard_map/by_weights/pallas_call | solution.py:414
  456.6 36.6 %hidden.7 = (bf16[4096,1024]{1,0:T(8,128)(2,1)}, bf16[4096,1024]{1,0:T(8,128)(2,1)}, bf16[4096,1024]{1,0:T(8,128)(2,1)}) custom-call(bf16[4096,1024]{1,0:T(8,128)(2,1)} %get-tuple-element.141.refs_0_.a, bf16[4096,1024]{1,0:T(8,128)(2,1)} %bitcast.58, bf16[1024,1024]{1,0:T(8,128)(2,1)} %get-tuple-element.154.wg.refs_11_, ...), custom_call_target="tpu_custom_call" | custom-call | flops 25769803776 | bytes 25165824 | tf_op jit(solution)/shard_map/hidden/pallas_call | solution.py:300
  493.2 37.3 %by_weights.4 = bf16[4,1,3,256,1024]{4,3,2,1,0:T(8,128)(2,1)} custom-call(bf16[4096,1024]{1,0:T(8,128)(2,1)} %bitcast.59, bf16[4096,1024]{1,0:T(8,128)(2,1)} %get-tuple-element.141.refs_0_.a, bf16[4096,1024]{1,0:T(8,128)(2,1)} %get-tuple-element.170.refs_0_, bf16[4096,1024]{1,0:T(8,128)(2,1)} %get-tuple-element.157.refs_3_.refs_1_, ...), custom_call_target="tpu_custom_call" | custom-call | flops 25769803776 | bytes 41943040 | tf_op jit(solution)/shard_map/by_weights/pallas_call | solution.py:414
  530.6 90.1 %by_input.1.dh = bf16[4096,1024]{1,0:T(8,128)(2,1)} custom-call(bf16[4096,1024]{1,0:T(8,128)(2,1)} %get-tuple-element.140.h, bf16[4096,1024]{1,0:T(8,128)(2,1)} %bitcast.60, bf16[4096,1024]{1,0:T(8,128)(2,1)} %get-tuple-element.145.refs_0_.refs_1_, bf16[4096,1024]{1,0:T(8,128)(2,1)} %get-tuple-element.149.refs_1_, ...), custom_call_target="tpu_custom_call" | custom-call | flops 68719476736 | bytes 67108864 | tf_op jit(solution)/shard_map/by_input/pallas_call | solution.py:450
  620.7 51.2 %first_back.7 = bf16[4,1,3,256,1024]{4,3,2,1,0:T(8,128)(2,1)} custom-call(bf16[4096,1024]{1,0:T(8,128)(2,1)} %by_input.1.dh, bf16[4096,1024]{1,0:T(8,128)(2,1)} %get-tuple-element.126.refs_0_.a, bf16[1024,1024]{1,0:T(8,128)(2,1)} %get-tuple-element.136.refs_5_.wd, f32[4096,1024]{1,0:T(8,128)} %get-tuple-element.168.gate, ...), custom_call_target="tpu_custom_call" | custom-call | flops 34359738368 | bytes 41943040 | tf_op jit(solution)/shard_map/first_back/pallas_call | solution.py:355
  672.0 50.7 %first_back.6 = bf16[4,1,3,256,1024]{4,3,2,1,0:T(8,128)(2,1)} custom-call(bf16[4096,1024]{1,0:T(8,128)(2,1)} %by_input.1.dh, bf16[4096,1024]{1,0:T(8,128)(2,1)} %get-tuple-element.126.refs_0_.a, bf16[1024,1024]{1,0:T(8,128)(2,1)} %get-tuple-element.137.refs_6_.wd, f32[4096,1024]{1,0:T(8,128)} %get-tuple-element.166.gate, ...), custom_call_target="tpu_custom_call" | custom-call | flops 34359738368 | bytes 41943040 | tf_op jit(solution)/shard_map/first_back/pallas_call | solution.py:355
  722.9 50.8 %first_back.5 = bf16[4,1,3,256,1024]{4,3,2,1,0:T(8,128)(2,1)} custom-call(bf16[4096,1024]{1,0:T(8,128)(2,1)} %by_input.1.dh, bf16[4096,1024]{1,0:T(8,128)(2,1)} %get-tuple-element.126.refs_0_.a, bf16[1024,1024]{1,0:T(8,128)(2,1)} %get-tuple-element.138.refs_7_.wd, f32[4096,1024]{1,0:T(8,128)} %get-tuple-element.164.gate, ...), custom_call_target="tpu_custom_call" | custom-call | flops 34359738368 | bytes 41943040 | tf_op jit(solution)/shard_map/first_back/pallas_call | solution.py:355
  773.9 50.6 %first_back.4 = bf16[4,1,3,256,1024]{4,3,2,1,0:T(8,128)(2,1)} custom-call(bf16[4096,1024]{1,0:T(8,128)(2,1)} %by_input.1.dh, bf16[4096,1024]{1,0:T(8,128)(2,1)} %get-tuple-element.126.refs_0_.a, bf16[1024,1024]{1,0:T(8,128)(2,1)} %get-tuple-element.139.refs_8_.wd, f32[4096,1024]{1,0:T(8,128)} %get-tuple-element.162.gate, ...), custom_call_target="tpu_custom_call" | custom-call | flops 34359738368 | bytes 41943040 | tf_op jit(solution)/shard_map/first_back/pallas_call | solution.py:355
  832.0 7.4 adamw.9
  839.5 7.4 adamw.10
  846.9 7.4 adamw.11
  861.8 7.4 adamw.13
  876.7 41.5 %reduce-scatter.9.cloned.1.call-done = bf16[768,1024]{1,0:T(8,128)(2,1)} async-done(((bf16[3072,1024]{1,0:T(8,128)(2,1)}), bf16[768,1024]{1,0:T(8,128)(2,1)}) %reduce-scatter.9.cloned.1.call-update) | async-done | bytes 1572880 | tf_op jit(solution)/shard_map/reduce_scatter | solution.py:511
  (27 shorter events, 30.6 us)
Async XLA Ops:
  7.2 817.4 %reduce-scatter.23.cloned.1.call-start = ((), (), s32[]{:S(2)}) async-start(), calls=%async_computation.15 | async-start | bytes 7864320 | tf_op jit(solution)/shard_map/reduce_scatter | solution.py:511
  381.5 450.5 %reduce-scatter.21.cloned.1.call-start = ((), (), s32[]{:S(2)}) async-start(), calls=%async_computation.14 | async-start | bytes 7864320 | tf_op jit(solution)/shard_map/reduce_scatter | solution.py:511
  418.9 420.6 %reduce-scatter.19.cloned.1.call-start = ((), (), s32[]{:S(2)}) async-start(), calls=%async_computation.13 | async-start | bytes 7864320 | tf_op jit(solution)/shard_map/reduce_scatter | solution.py:511
  456.5 390.4 %reduce-scatter.17.cloned.1.call-start = ((), (), s32[]{:S(2)}) async-start(), calls=%async_computation.12 | async-start | bytes 7864320 | tf_op jit(solution)/shard_map/reduce_scatter | solution.py:511
  530.6 323.8 %reduce-scatter.15.cloned.1.call-start = ((), (), s32[]{:S(2)}) async-start(), calls=%async_computation.11 | async-start | bytes 7864320 | tf_op jit(solution)/shard_map/reduce_scatter | solution.py:511
  672.0 189.8 %reduce-scatter.13.cloned.1.call-start = ((), (), s32[]{:S(2)}) async-start(), calls=%async_computation.10 | async-start | bytes 7864320 | tf_op jit(solution)/shard_map/reduce_scatter | solution.py:511
  722.8 146.4 %reduce-scatter.11.cloned.1.call-start = ((), (), s32[]{:S(2)}) async-start(), calls=%async_computation.9 | async-start | bytes 7864320 | tf_op jit(solution)/shard_map/reduce_scatter | solution.py:511
  773.8 144.3 %reduce-scatter.9.cloned.1.call-start = ((), (), s32[]{:S(2)}) async-start(), calls=%async_computation.8 | async-start | bytes 7864320 | tf_op jit(solution)/shard_map/reduce_scatter | solution.py:511
Sparse Core Ops, SparseCore 0:
  381.6 60.3 reduce-scatter.22
  444.3 59.5 reduce-scatter.20
  506.3 59.5 reduce-scatter.18
  568.0 59.6 reduce-scatter.16
  672.1 60.3 reduce-scatter.14
  734.6 59.5 reduce-scatter.12
  796.6 59.5 reduce-scatter.10
  858.5 59.6 reduce-scatter.8
